TPU v7x, 768 devices: a whole 4x8x12 slice. The times are simulated.
768 devices in a mesh: section: 192 (over x, y_lo, z), tensor: 4 (over y_hi, core).
Axes of the slice: x: 4, y: 8 (y_hi: 2, y_lo: 4; y = y_hi * 4 + y_lo), z: 12, core: 2. Of those that a mesh axis runs over, the one named last changes fastest.
Arguments:
- hidden: bfloat16 [24576, 12288], P('section', 'tensor'), may hold values from -6 to 6
- cotangent: bfloat16 [24576, 12288], P('section', 'tensor'), may hold values from -6 to 6
- encoder: bfloat16 [12288, 1536], P('tensor'), may hold values from -0.0546875 to 0.0546875
- lengths: int32 [192], P('section'), may hold values from 64 to 128
Outputs:
- decoded: bfloat16 [24576, 12288], P('section', 'tensor')
- hidden_gradient: bfloat16 [24576, 12288], P('section', 'tensor')
All inputs are finite; a program needn't handle non-finite values.
Results may differ from a plain program's by a relative error of at most 0.0083.
Values may be sent and summed in bfloat16 or wider, within the bound.
A program may use at most 32 MiB of HBM per device.

v0:
```python
import jax
import jax.numpy as jnp
from jax import lax
from jax.sharding import PartitionSpec as P

MODEL_WIDTH = 12288


EPS = 1e-05


def copy_for_each(array, axis):
    copies = jnp.broadcast_to(array, (lax.axis_size(axis), *array.shape))
    return lax.all_to_all(copies, axis, split_axis=0, concat_axis=0, tiled=True)


def over_copies(array, axis):
    return copy_for_each(array, axis).sum(axis=0)


def in_one(arrays, axis):
    ends = [0]
    for a in arrays:
        ends.append(ends[-1] + a.size)
    subtotal = over_copies(jnp.concatenate([a.ravel() for a in arrays]), axis)
    return tuple((subtotal[b:e].reshape(a.shape) for a, b, e in zip(arrays, ends, ends[1:])))


def cut_along(array, dim, size):
    shape = array.shape
    pieces = array.reshape(*shape[:dim], size, shape[dim] // size, *shape[dim + 1 :])
    return jnp.moveaxis(pieces, dim, 0)


def sum_at_owner(array, axis, dim):
    pieces = cut_along(array, dim, lax.axis_size(axis))
    arrived = lax.all_to_all(pieces, axis, split_axis=0, concat_axis=0, tiled=True)
    return arrived.astype(jnp.float32).sum(axis=0)


def sent_together(arrays, axis, dim, along):
    both = jnp.concatenate(arrays, axis=along)
    out, at, outs = (sum_at_owner(both, axis, dim), 0, [])
    for a in arrays:
        outs.append(lax.slice_in_dim(out, at, at + a.shape[along], axis=along))
        at += a.shape[along]
    return tuple(outs)


def shifted(block, axis, distance):
    devices = range(lax.axis_size(axis))
    route = [((i - distance) % len(devices), i) for i in devices]
    return lax.ppermute(block, axis, route)


def in_one_2(arrays, axis):
    ends = [0]
    for a in arrays:
        ends.append(ends[-1] + a.size)
    subtotal = lax.psum(jnp.concatenate([a.ravel() for a in arrays]), axis)
    return tuple((subtotal[b:e].reshape(a.shape) for a, b, e in zip(arrays, ends, ends[1:])))


def times_transpose(left, encoder):
    return lax.dot_general(
        left, encoder, (((1,), (1,)), ((), ())), preferred_element_type=jnp.float32
    )


def shards(hidden, cotangent, encoder, lengths):
    value_entries = hidden.astype(jnp.float32)
    row_sum = jnp.sum(value_entries, axis=1)
    row_square = jnp.sum(value_entries * value_entries, axis=1)
    col_terms = jnp.sum(encoder.astype(jnp.float32), axis=0)
    grad_terms = jnp.dot(cotangent, encoder, preferred_element_type=jnp.float32)
    latent_terms = jnp.dot(hidden, encoder, preferred_element_type=jnp.float32)
    position = jnp.arange(hidden.shape[0], dtype=jnp.int32)
    mask = (position < lengths[0]).astype(jnp.float32)[:, None]
    total, square, colsum_full = in_one((row_sum, row_square, col_terms), "tensor")
    grad_share, latent_share = sent_together(
        (grad_terms.astype(jnp.bfloat16), latent_terms.astype(jnp.bfloat16)), "tensor", 1, 0
    )
    share_width = latent_share.shape[1]
    colsum = lax.dynamic_slice_in_dim(
        colsum_full, lax.axis_index("tensor") * share_width, share_width, 0
    )
    row_average = (total / MODEL_WIDTH)[:, None]
    meansq = (square / MODEL_WIDTH)[:, None]
    inverse_deviation = lax.rsqrt(meansq - row_average * row_average + EPS)
    normalized_input = (value_entries - row_average) * inverse_deviation
    latent = (mask * inverse_deviation * (latent_share - row_average * colsum[None, :])).astype(
        jnp.bfloat16
    )
    arrived = shifted(latent, "section", 1)
    received = lax.all_gather(arrived, "tensor", axis=1, tiled=True)
    returned = shifted(grad_share.astype(jnp.bfloat16), "section", -1)
    back = lax.all_gather(returned, "tensor", axis=1, tiled=True)
    decoded = times_transpose(received, encoder).astype(jnp.bfloat16)
    back = back * mask.astype(jnp.bfloat16)
    normalized_gradient = times_transpose(back, encoder)
    first_piece, second_piece = in_one_2(
        (
            jnp.sum(normalized_gradient, axis=1),
            jnp.sum(normalized_gradient * normalized_input, axis=1),
        ),
        "tensor",
    )
    hidden_gradient = inverse_deviation * (
        normalized_gradient
        - (first_piece / MODEL_WIDTH)[:, None]
        - normalized_input * (second_piece / MODEL_WIDTH)[:, None]
    )
    return (decoded, hidden_gradient.astype(jnp.bfloat16))


def solution(mesh):
    return jax.shard_map(
        shards,
        mesh=mesh,
        in_specs=(P("section", "tensor"), P("section", "tensor"), P("tensor", None), P("section")),
        out_specs=(P("section", "tensor"), P("section", "tensor")),
        check_vma=False,
    )
```

profile of v0, /device:TPU:59, one launch (start us, length us, event | category | flops | bytes accessed | tf_op | source)
XLA Modules:
  0.0 122.5 jit_solution(17006882409629242659)
XLA Ops:
  0.6 0.0 copy-start
  0.6 1.5 %convert_reduce_fusion.1 = (f32[128]{0:T(128)S(1)}, f32[128]{0:T(128)S(1)}) fusion(bf16[128,3072]{1,0:T(8,128)(2,1)} %param.4), kind=kLoop, calls=%fused_computation.6 | loop fusion | flops 1572608 | bytes 787456 | tf_op jit(solution)/shard_map/reduce_sum | solution.py:72
  2.1 0.0 copy-start.1
  2.1 5.1 %convert_reduce_fusion = f32[1536]{0:T(1024)S(1)} fusion(bf16[3072,1536]{1,0:T(8,128)(2,1)} %param.6), kind=kLoop, calls=%fused_computation | loop fusion | flops 9435648 | bytes 9443328 | tf_op jit(solution)/shard_map/reduce_sum | solution.py:74
  7.3 0.6 broadcast_in_dim.2
  7.9 7.5 %all-to-all-start = ((f32[4,1,1792]{2,1,0:T(1,128)}), f32[4,1,1792]{2,1,0:T(1,128)S(1)}, u32[]{:S(2)}, u32[]{:S(2)}) async-start(f32[4,1,1792]{2,1,0:T(1,128)} %broadcast_in_dim.2), calls=%async_computation | async-start | bytes 57344 | tf_op jit(solution)/shard_map/all_to_all | solution.py:14
  15.4 0.0 copy-done.1
  15.4 5.1 %convolution_convert_fusion.1 = bf16[128,1536]{1,0:T(8,128)(2,1)S(1)} fusion(bf16[128,3072]{1,0:T(8,128)(2,1)S(1)} %copy-done.1, bf16[3072,1536]{1,0:T(8,128)(2,1)} %param.6), kind=kOutput, calls=%fused_computation.2 | convolution fusion | flops 1208156160 | bytes 10616832 | tf_op jit(solution)/shard_map/dot_general | solution.py:76
  20.4 0.0 copy-done
  20.5 5.1 %convolution_convert_fusion.2 = bf16[128,1536]{1,0:T(8,128)(2,1)S(1)} fusion(bf16[128,3072]{1,0:T(8,128)(2,1)S(1)} %copy-done, bf16[3072,1536]{1,0:T(8,128)(2,1)} %param.6), kind=kOutput, calls=%fused_computation.3 | convolution fusion | flops 1208156160 | bytes 10616832 | tf_op jit(solution)/shard_map/dot_general | solution.py:75
  25.5 0.1 pad_maximum_fusion
  25.6 1.0 copy.17
  26.6 0.0 all-to-all-done
  26.6 7.2 %all-to-all-start.1 = ((bf16[4,256,384]{2,1,0:T(8,128)(2,1)}), bf16[4,256,384]{2,1,0:T(8,128)(2,1)S(1)}, u32[]{:S(2)}, u32[]{:S(2)}) async-start(bf16[4,256,384]{2,1,0:T(8,128)(2,1)} %bitcast.14), calls=%async_computation.1 | async-start | bytes 1572864 | tf_op jit(solution)/shard_map/all_to_all | solution.py:37
  34.5 0.1 dynamic_slice.3
  34.6 9.3 %all-to-all-done.1 = bf16[4,256,384]{2,1,0:T(8,128)(2,1)S(1)} async-done(((bf16[4,256,384]{2,1,0:T(8,128)(2,1)}), bf16[4,256,384]{2,1,0:T(8,128)(2,1)S(1)}, u32[]{:S(2)}, u32[]{:S(2)}) %all-to-all-start.1) | async-done | bytes 786464 | tf_op jit(solution)/shard_map/all_to_all | solution.py:37
  43.9 0.1 convert_reduce_fusion.2
  44.0 23.4 %collective-permute-start.1 = (bf16[128,384]{1,0:T(8,128)(2,1)S(1)}, bf16[128,384]{1,0:T(8,128)(2,1)S(1)}, u32[]{:S(2)}, u32[]{:S(2)}) collective-permute-start(bf16[128,384]{1,0:T(8,128)(2,1)S(1)} %slice.50), channel_id=1, source_target_pairs={{4,0},{8,4},{12,8},{16,12},{20,16},{24,20},{28,24},{32,28},{36,32}... | collective-permute-start | bytes 294920 | tf_op jit(solution)/shard_map/ppermute | solution.py:53
  67.4 0.1 fusion.11
  67.5 1.9 %collective-permute-start = (bf16[128,384]{1,0:T(8,128)(2,1)S(1)}, bf16[128,384]{1,0:T(8,128)(2,1)S(1)}, u32[]{:S(2)}, u32[]{:S(2)}) collective-permute-start(bf16[128,384]{1,0:T(8,128)(2,1)S(1)} %fusion.11), channel_id=1, source_target_pairs={{764,0},{0,4},{4,8},{8,12},{12,16},{16,20},{20,24},{24,28},{28,32}... | collective-permute-start | bytes 294920 | tf_op jit(solution)/shard_map/ppermute | solution.py:53
  69.5 0.0 collective-permute-done.1
  69.5 12.8 %all_gather.7 = bf16[128,1536]{1,0:T(8,128)(2,1)S(1)} all-gather(bf16[128,384]{1,0:T(8,128)(2,1)S(1)} %collective-permute-done.1), channel_id=1, replica_groups=mesh['section'=192,'tensor'=4] {'tensor'}, dimensions={1}, use_global_device_ids=true | all-gather | bytes 491520 | tf_op jit(solution)/shard_map/all_gather | solution.py:97
  82.3 7.0 %fusion.15 = (f32[128]{0:T(128)S(1)}, f32[128]{0:T(128)S(1)}, f32[128,3072]{1,0:T(8,128)S(1)}) fusion(f32[128]{0:T(128)S(1)} %get-tuple-element.7, f32[128]{0:T(128)S(1)} %get-tuple-element.8, bf16[128,3072]{1,0:T(8,128)(2,1)S(1)} %copy-done.1, bf16[3072,1536]{1,0:T(8,128)(2,1)} %param.6, bf16[128,1536]{1,0:T(8,128)(2,1)S(1)} %all_gather.7, ...), kind=kOutput, calls=%fused_computation.36 | convolution fusion | flops 1210515200 | bytes 12192000 | tf_op jit(solution)/shard_map/dot_general | solution.py:65
  89.3 9.1 %psum.7 = f32[256]{0:T(256)S(1)} all-reduce(f32[256]{0:T(256)S(1)} %pad_maximum_fusion.2), channel_id=1, replica_groups=mesh['section'=192,'tensor'=4] {'tensor'}, use_global_device_ids=true, to_apply=%region_7.0 | all-reduce | flops 256 | bytes 2048 | tf_op jit(solution)/shard_map/psum | solution.py:60
  98.4 0.0 collective-permute-done
  98.4 14.9 %all_gather.6 = bf16[128,1536]{1,0:T(8,128)(2,1)S(1)} all-gather(bf16[128,384]{1,0:T(8,128)(2,1)S(1)} %collective-permute-done), channel_id=1, replica_groups=mesh['section'=192,'tensor'=4] {'tensor'}, dimensions={1}, use_global_device_ids=true | all-gather | bytes 491520 | tf_op jit(solution)/shard_map/all_gather | solution.py:95
  113.3 7.7 %convolution_convert_fusion = bf16[128,3072]{1,0:T(8,128)(2,1)} fusion(bf16[128,1536]{1,0:T(8,128)(2,1)S(1)} %all_gather.6, bf16[3072,1536]{1,0:T(8,128)(2,1)} %param.6), kind=kOutput, calls=%fused_computation.1 | convolution fusion | flops 1208352768 | bytes 10616832 | tf_op jit(solution)/shard_map/dot_general | solution.py:65
  121.0 1.4 %fusion.7 = bf16[128,3072]{1,0:T(8,128)(2,1)} fusion(bf16[128,3072]{1,0:T(8,128)(2,1)S(1)} %copy-done.1, f32[128,3072]{1,0:T(8,128)S(1)} %get-tuple-element.11, f32[128]{0:T(128)S(1)} %get-tuple-element.10, f32[128]{0:T(128)S(1)} %get-tuple-element.9, f32[128]{0:T(128)S(1)} %get-tuple-element.8, f32[128]{0:T(128)S(1)} %get-tuple-element.7), kind=kLoop, calls=%fused_computation.14 | loop fusion | flops 3145728 | bytes 3147776 | tf_op jit(solution)/shard_map/convert_element_type | solution.py:113
  (8 shorter events, 0.1 us)
Async XLA Ops:
  0.6 19.8 %copy-start = (bf16[128,3072]{1,0:T(8,128)(2,1)S(1)}, bf16[128,3072]{1,0:T(8,128)(2,1)}, u32[]{:S(2)}) copy-start(bf16[128,3072]{1,0:T(8,128)(2,1)} %param.5) | copy-start | bytes 2359300
  2.1 13.2 %copy-start.1 = (bf16[128,3072]{1,0:T(8,128)(2,1)S(1)}, bf16[128,3072]{1,0:T(8,128)(2,1)}, u32[]{:S(2)}) copy-start(bf16[128,3072]{1,0:T(8,128)(2,1)} %param.4) | copy-start | bytes 2359300
  7.9 18.7 %all-to-all-start = ((f32[4,1,1792]{2,1,0:T(1,128)}), f32[4,1,1792]{2,1,0:T(1,128)S(1)}, u32[]{:S(2)}, u32[]{:S(2)}) async-start(f32[4,1,1792]{2,1,0:T(1,128)} %broadcast_in_dim.2), calls=%async_computation | async-start | bytes 57344 | tf_op jit(solution)/shard_map/all_to_all | solution.py:14
  26.6 17.3 %all-to-all-start.1 = ((bf16[4,256,384]{2,1,0:T(8,128)(2,1)}), bf16[4,256,384]{2,1,0:T(8,128)(2,1)S(1)}, u32[]{:S(2)}, u32[]{:S(2)}) async-start(bf16[4,256,384]{2,1,0:T(8,128)(2,1)} %bitcast.14), calls=%async_computation.1 | async-start | bytes 1572864 | tf_op jit(solution)/shard_map/all_to_all | solution.py:37
  44.0 25.4 %collective-permute-start.1 = (bf16[128,384]{1,0:T(8,128)(2,1)S(1)}, bf16[128,384]{1,0:T(8,128)(2,1)S(1)}, u32[]{:S(2)}, u32[]{:S(2)}) collective-permute-start(bf16[128,384]{1,0:T(8,128)(2,1)S(1)} %slice.50), channel_id=1, source_target_pairs={{4,0},{8,4},{12,8},{16,12},{20,16},{24,20},{28,24},{32,28},{36,32}... | collective-permute-start | bytes 294920 | tf_op jit(solution)/shard_map/ppermute | solution.py:53
  67.5 30.9 %collective-permute-start = (bf16[128,384]{1,0:T(8,128)(2,1)S(1)}, bf16[128,384]{1,0:T(8,128)(2,1)S(1)}, u32[]{:S(2)}, u32[]{:S(2)}) collective-permute-start(bf16[128,384]{1,0:T(8,128)(2,1)S(1)} %fusion.11), channel_id=1, source_target_pairs={{764,0},{0,4},{4,8},{8,12},{12,16},{16,20},{20,24},{24,28},{28,32}... | collective-permute-start | bytes 294920 | tf_op jit(solution)/shard_map/ppermute | solution.py:53
where the time goes:
time: 123 us; the launch traced here: 122 us
  starting transfers between devices  40 us (33%)
  blocking collectives  36.9 us (30%)
  matrix products  24.8 us (20%)
  waiting for transfers between devices  9.33 us (8%)
  other arithmetic  8.34 us (7%)
  local copies, waits for them, and re-layouts  1.7 us (1%)
  between operations  1.41 us (1%)
    ppermute x2, starting transfers between devices, shifted(): return lax.ppermute(block, axis, route)  25.3 us
    all_gather x1, blocking collectives, shards(): received = lax.all_gather(arrived, 'tensor', axis=1, tiled=True)  14.9 us
    dot_general x2, matrix products, times_transpose(): lax.dot_general(left, encoder, (((1,), (1,)), ((), ())), preferred_elemen...  14.7 us
    all_gather x1, blocking collectives, shards(): back = lax.all_gather(returned, 'tensor', axis=1, tiled=True)  12.8 us
    all_to_all x1, waiting for transfers between devices, sum_at_owner(): lax.all_to_all(pieces, axis, split_axis=0, concat_axis=0, tiled=True)  9.33 us
    psum x1, blocking collectives, in_one_2(): subtotal = lax.psum(jnp.concatenate([a.ravel() for a in arrays]), axis)  9.1 us
    all_to_all x1, starting transfers between devices, copy_for_each(): return lax.all_to_all(copies, axis, split_axis=0, concat_axis=0, tiled=True)  7.48 us
    all_to_all x1, starting transfers between devices, sum_at_owner(): lax.all_to_all(pieces, axis, split_axis=0, concat_axis=0, tiled=True)  7.2 us
  transfers between devices with their start and end apart: 4, of which 1 were waited for; matrix products, arithmetic and copies ran while one was open for 15% of the time, Pallas kernels for 0%

commit v1 on v0

v1 whole, which is shorter than its diff:
```python
import functools

import jax
import jax.numpy as jnp
from jax import lax
from jax.experimental import pallas as pl
from jax.experimental.pallas import tpu as pltpu
from jax.sharding import PartitionSpec as P

MODEL_WIDTH = 12288
EPS = 1e-05
MESH = pl.DeviceIdType.MESH
F32 = jnp.float32
BF16 = jnp.bfloat16

ROWS = 128
DEPTH = 3072
BLOCK = 256
HALF = 128
PER = 3
BLOCKS = 2 * PER
SPLIT = 4
CHUNK = DEPTH // SPLIT


def column(row):
    return jnp.broadcast_to(row, (ROWS, HALF)).T


def row_of(square):
    return jnp.sum(square.T, axis=0, keepdims=True)


def kernel(
    sections,
    hidden,
    cotangent,
    encoder,
    lengths,
    decoded,
    gradient,
    x,
    enc,
    part,
    part_in,
    colsum,
    ys,
    yr,
    gs,
    ls,
    zs,
    back,
    recv,
    stat_out,
    stat_in,
    piece_out,
    piece_in,
    acc_b,
    acc_r,
    out_d,
    out_g,
    load_sem,
    part_ss,
    part_rs,
    y_ss,
    y_rs,
    stat_ss,
    stat_rs,
    shift_ss,
    shift_rs,
    gy_ss,
    gy_rs,
    gd_ss,
    gd_rs,
    gf_ss,
    gf_rs,
    piece_ss,
    piece_rs,
    out_sem,
):
    s = lax.axis_index("section")
    t = lax.axis_index("tensor")
    c = lax.rem(t, 2)
    chip = t // 2
    t_core = chip * 2 + (1 - c)
    t_far = (1 - chip) * 2 + c
    t_diag = (1 - chip) * 2 + (1 - c)
    core = {"section": s, "tensor": t_core}
    far = {"section": s, "tensor": t_far}
    diag = {"section": s, "tensor": t_diag}
    after = {"section": lax.rem(s + 1, sections), "tensor": t}
    before = {"section": lax.rem(s + sections - 1, sections), "tensor": t}
    peers = (core, far, diag)

    def remote(src, dst, ss, rs, to):
        return pltpu.make_async_remote_copy(
            src_ref=src, dst_ref=dst, send_sem=ss, recv_sem=rs, device_id=to, device_id_type=MESH
        )

    def load_encoder(p):
        b = lax.rem(PER * (1 - chip) + p, BLOCKS)
        at = pl.ds(pl.multiple_of(b * BLOCK, BLOCK), BLOCK)
        return pltpu.make_async_copy(encoder.at[:, at], enc.at[p], load_sem.at[2 + p])

    load_c = pltpu.make_async_copy(cotangent, x.at[pl.ds(0, ROWS)], load_sem.at[0])
    load_h = pltpu.make_async_copy(hidden, x.at[pl.ds(ROWS, ROWS)], load_sem.at[1])

    def send_part(p):
        return remote(part.at[p, 1 - c], part_in.at[p], part_ss.at[p], part_rs.at[p], core)

    def send_far(a, j):
        i = a * PER + j
        return remote(ys.at[i], yr.at[i], y_ss.at[i], y_rs.at[i], far)

    def send_stat(k):
        return remote(stat_out.at[k], stat_in.at[k], stat_ss.at[k], stat_rs.at[k], peers[k])

    def send_piece(k):
        return remote(piece_out, piece_in.at[k], piece_ss.at[k], piece_rs.at[k], peers[k])

    def shift(a, j):
        i = a * PER + j
        src, dst, to = ((gs, back, before), (ls, recv, after))[a]
        return remote(src.at[j], dst.at[PER + j, c], shift_ss.at[i], shift_rs.at[i], to)

    def gather_far(a, j):
        i = a * PER + j
        buf = (back, recv)[a]
        return remote(buf.at[PER + j, c], buf.at[j, c], gy_ss.at[i], gy_rs.at[i], far)

    def gather_core(a, j):
        i = a * PER + j
        buf = (back, recv)[a]
        return remote(buf.at[PER + j, c], buf.at[PER + j, c], gd_ss.at[i], gd_rs.at[i], core)

    def pass_core(a, j):
        i = a * PER + j
        buf = (back, recv)[a]
        return remote(buf.at[j, c], buf.at[j, c], gf_ss.at[i], gf_rs.at[i], core)

    def loop(body):
        def step(j, carry):
            body(j)
            return carry

        lax.fori_loop(0, PER, step, 0)

    load_h.start()
    load_c.start()
    load_encoder(0).start()
    load_encoder(1).start()
    barrier = pltpu.get_barrier_semaphore()
    for to in (core, far, diag, after, before):
        pl.semaphore_signal(barrier, inc=1, device_id=to, device_id_type=MESH)
    x[pl.ds(2 * ROWS, 16), :] = jnp.ones((16, DEPTH), BF16)

    load_h.wait()
    total = jnp.zeros((ROWS, HALF), F32)
    square = jnp.zeros((ROWS, HALF), F32)
    for i in range(DEPTH // HALF):
        v = x[ROWS : 2 * ROWS, i * HALF : (i + 1) * HALF].astype(F32)
        total = total + v
        square = square + v * v
    total = row_of(total)
    square = row_of(square)
    own_mean = total / DEPTH
    mean_here = column(own_mean)
    stat_out[...] = jnp.zeros(stat_out.shape, F32)
    for k in range(4):
        stat_out[k, 3:4, :] = total
        stat_out[k, 4:5, :] = square
    load_c.wait()

    def encode(p):
        load_encoder(p).wait()
        y = jnp.dot(x[...], enc[p], preferred_element_type=F32)
        for h in range(2):
            at = slice(h * HALF, (h + 1) * HALF)
            cs = y[2 * ROWS : 2 * ROWS + 1, at]
            part[p, h, 0:ROWS, :] = y[0:ROWS, at]
            part[p, h, ROWS : 2 * ROWS, :] = y[ROWS : 2 * ROWS, at] - mean_here * cs
            colsum[p, h] = y[2 * ROWS : 2 * ROWS + 8, at]

    def first_blocks(j):
        load_encoder(j + 2).start()
        encode(j)

    loop(first_blocks)
    load_encoder(PER + 2).start()
    pl.semaphore_wait(barrier, 5)

    def start_parts(j):
        send_part(j).start()

    loop(start_parts)

    def last_blocks(j):
        encode(PER + j)
        send_part(PER + j).start()
        send_part(j).wait_recv()
        total_here = part[j, c] + part_in[j]
        ys[j] = total_here[0:ROWS].astype(BF16)
        ys[PER + j] = total_here[ROWS : 2 * ROWS].astype(BF16)
        send_far(0, j).start()

    loop(last_blocks)

    for j in range(PER):
        stat_out[0, j : j + 1, :] = colsum[PER + j, 1 - c][0:1]
        stat_out[1, j : j + 1, :] = colsum[j, c][0:1]
        stat_out[2, j : j + 1, :] = colsum[j, 1 - c][0:1]
        stat_out[3, j : j + 1, :] = colsum[PER + j, c][0:1]
    for k in range(3):
        send_stat(k).start()

    def start_second(j):
        send_far(1, j).start()

    loop(start_second)

    def finish_grad(j):
        send_part(PER + j).wait_recv()
        send_far(0, j).wait_recv()
        full = part[PER + j, c, 0:ROWS, :] + part_in[PER + j, 0:ROWS, :] + yr[j].astype(F32)
        gs[j] = full.astype(BF16)
        shift(0, j).start()

    loop(finish_grad)

    for k in range(3):
        send_stat(k).wait_recv()
    shares = [stat_in[0], stat_in[1], stat_in[2], stat_out[3]]
    tile = shares[0] + shares[1] + shares[2] + shares[3]
    mean_row = tile[3:4] / MODEL_WIDTH
    meansq = tile[4:5] / MODEL_WIDTH
    rstd_row = lax.rsqrt(meansq - mean_row * mean_row + EPS)
    mean = column(mean_row)
    rstd = column(rstd_row)
    offsets = [column(v[3:4] / DEPTH - mean_row) for v in shares]
    real = lengths[0]
    mask = (lax.broadcasted_iota(jnp.int32, (ROWS, HALF), 0) < real).astype(F32)
    mask_row = (lax.broadcasted_iota(jnp.int32, (1, HALF), 1) < real).astype(F32)

    first = jnp.zeros((ROWS, HALF), F32)
    second = jnp.zeros((ROWS, HALF), F32)
    for j in range(PER):
        send_far(1, j).wait_recv()
        full = (
            part[PER + j, c, ROWS : 2 * ROWS, :]
            + part_in[PER + j, ROWS : 2 * ROWS, :]
            + yr[PER + j].astype(F32)
        )
        for v, o in zip(shares, offsets):
            full = full + o * v[j : j + 1]
        z = rstd * full
        zs[j] = z
        ls[j] = (mask * z).astype(BF16)
        shift(1, j).start()
        shift(0, j).wait_recv()
        gather_far(0, j).start()
        gather_core(0, j).start()
    for j in range(PER):
        b = back[PER + j, c].astype(F32)
        first = first + b * tile[j : j + 1]
        second = second + b * zs[j]
    piece_out[...] = jnp.zeros(piece_out.shape, F32)
    piece_out[0:1, :] = row_of(first) * mask_row
    piece_out[1:2, :] = row_of(second) * mask_row
    for k in range(3):
        send_piece(k).start()

    def decode(acc, buf, p, fresh):
        left = jnp.concatenate([buf[p, 0], buf[p, 1]], axis=1)

        def step(n, carry):
            at = pl.ds(pl.multiple_of(n * CHUNK, CHUNK), CHUNK)
            d = lax.dot_general(
                left, enc[p, at, :], (((1,), (1,)), ((), ())), preferred_element_type=F32
            )
            acc[n] = acc[n] + d
            return carry

        lax.fori_loop(0, SPLIT, step, 0)

    acc_b[...] = jnp.zeros(acc_b.shape, F32)
    acc_r[...] = jnp.zeros(acc_r.shape, F32)

    def middle(j):
        shift(1, j).wait_recv()
        gather_far(1, j).start()
        gather_core(1, j).start()
        gather_core(0, j).wait_recv()
        decode(acc_b, back, PER + j, False)
        gather_far(0, j).wait_recv()
        pass_core(0, j).start()

    loop(middle)

    def late(j):
        pass_core(0, j).wait_recv()
        decode(acc_b, back, j, False)
        gather_core(1, j).wait_recv()
        decode(acc_r, recv, PER + j, False)
        gather_far(1, j).wait_recv()
        pass_core(1, j).start()

    loop(late)

    for k in range(3):
        send_piece(k).wait_recv()
    pieces = piece_out[...] + piece_in[0] + piece_in[1] + piece_in[2]
    first = column(pieces[0:1] / MODEL_WIDTH)
    second = column(pieces[1:2] / MODEL_WIDTH)

    def to_gradient(n):
        at = pl.ds(pl.multiple_of(n * CHUNK, CHUNK), CHUNK)
        return pltpu.make_async_copy(out_g.at[n], gradient.at[:, at], out_sem.at[n])

    def to_decoded(n):
        at = pl.ds(pl.multiple_of(n * CHUNK, CHUNK), CHUNK)
        return pltpu.make_async_copy(out_d.at[n], decoded.at[:, at], out_sem.at[SPLIT + n])

    for n in range(SPLIT):
        for i in range(CHUNK // HALF):
            lo = n * CHUNK + i * HALF
            v = x[ROWS : 2 * ROWS, lo : lo + HALF].astype(F32)
            normed = (v - mean) * rstd
            g = acc_b[n, :, i * HALF : (i + 1) * HALF] * mask
            out_g[n, :, i * HALF : (i + 1) * HALF] = (
                rstd * (g - first - normed * second)
            ).astype(BF16)
        to_gradient(n).start()

    def final(j):
        pass_core(1, j).wait_recv()
        decode(acc_r, recv, j, False)

    loop(final)
    for n in range(SPLIT):
        out_d[n] = acc_r[n].astype(BF16)
        to_decoded(n).start()

    def drain(p, carry):
        send_part(p).wait_send()
        return carry

    lax.fori_loop(0, BLOCKS, drain, 0)

    def drain_rest(j):
        for a in range(2):
            send_far(a, j).wait_send()
            shift(a, j).wait_send()
            gather_far(a, j).wait_send()
            gather_core(a, j).wait_send()
            pass_core(a, j).wait_send()

    loop(drain_rest)
    for k in range(3):
        send_stat(k).wait_send()
        send_piece(k).wait_send()
    for n in range(SPLIT):
        to_gradient(n).wait()
        to_decoded(n).wait()


def shards(sections, hidden, cotangent, encoder, lengths):
    any_space = pl.BlockSpec(memory_space=pl.ANY)
    sems = lambda n: pltpu.SemaphoreType.DMA((n,))
    return pl.pallas_call(
        functools.partial(kernel, sections),
        out_shape=(
            jax.ShapeDtypeStruct((ROWS, DEPTH), BF16),
            jax.ShapeDtypeStruct((ROWS, DEPTH), BF16),
        ),
        in_specs=[any_space, any_space, any_space, pl.BlockSpec(memory_space=pltpu.SMEM)],
        out_specs=(any_space, any_space),
        scratch_shapes=[
            pltpu.VMEM((2 * ROWS + 16, DEPTH), BF16),
            pltpu.VMEM((BLOCKS, DEPTH, BLOCK), BF16),
            pltpu.VMEM((BLOCKS, 2, 2 * ROWS, HALF), F32),
            pltpu.VMEM((BLOCKS, 2 * ROWS, HALF), F32),
            pltpu.VMEM((BLOCKS, 2, 8, HALF), F32),
            pltpu.VMEM((2 * PER, ROWS, HALF), BF16),
            pltpu.VMEM((2 * PER, ROWS, HALF), BF16),
            pltpu.VMEM((PER, ROWS, HALF), BF16),
            pltpu.VMEM((PER, ROWS, HALF), BF16),
            pltpu.VMEM((PER, ROWS, HALF), F32),
            pltpu.VMEM((BLOCKS, 2, ROWS, HALF), BF16),
            pltpu.VMEM((BLOCKS, 2, ROWS, HALF), BF16),
            pltpu.VMEM((4, 8, HALF), F32),
            pltpu.VMEM((3, 8, HALF), F32),
            pltpu.VMEM((8, HALF), F32),
            pltpu.VMEM((3, 8, HALF), F32),
            pltpu.VMEM((SPLIT, ROWS, CHUNK), F32),
            pltpu.VMEM((SPLIT, ROWS, CHUNK), F32),
            pltpu.VMEM((SPLIT, ROWS, CHUNK), BF16),
            pltpu.VMEM((SPLIT, ROWS, CHUNK), BF16),
            sems(2 + BLOCKS),
            sems(BLOCKS),
            sems(BLOCKS),
            sems(2 * PER),
            sems(2 * PER),
            sems(3),
            sems(3),
            sems(2 * PER),
            sems(2 * PER),
            sems(2 * PER),
            sems(2 * PER),
            sems(2 * PER),
            sems(2 * PER),
            sems(2 * PER),
            sems(2 * PER),
            sems(3),
            sems(3),
            sems(2 * SPLIT),
        ],
        compiler_params=pltpu.CompilerParams(
            collective_id=0, has_side_effects=True, vmem_limit_bytes=48 * 1024 * 1024
        ),
        name="relay",
    )(hidden, cotangent, encoder, lengths)


def solution(mesh):
    return jax.shard_map(
        functools.partial(shards, mesh.shape["section"]),
        mesh=mesh,
        in_specs=(P("section", "tensor"), P("section", "tensor"), P("tensor", None), P("section")),
        out_specs=(P("section", "tensor"), P("section", "tensor")),
        check_vma=False,
    )
```

time: 123 us -> 59.1 us (0.48)
  the two profiles are of different devices: /device:TPU:59 before, /device:TPU:1 now
where the time goes in v1:
time: 59.1 us; the launch traced here: 58.9 us
  Pallas kernels  53.6 us (91%)
  local copies, waits for them, and re-layouts  4.02 us (7%)
  between operations  1.29 us (2%)
    pallas_call x1, Pallas kernels, shards(): pl.pallas_call(functools.partial(kernel, sections), out_shape=(jax.ShapeD...  53.6 us
    unnamed x6, local copies, waits for them, and re-layouts  4.02 us

profile of v1, /device:TPU:1, one launch (start us, length us, event | category | flops | bytes accessed | tf_op | source)
XLA Modules:
  0.0 58.9 jit_solution(3205938013295520296)
XLA Ops:
  1.3 0.0 copy-start
  1.3 1.1 %copy-done = bf16[128,3072]{1,0:T(8,128)(2,1)S(1)} copy-done((bf16[128,3072]{1,0:T(8,128)(2,1)S(1)}, bf16[128,3072]{1,0:T(8,128)(2,1)}, u32[]{:S(2)}) %copy-start) | copy-done | bytes 786456
  2.4 0.0 copy-start.1
  2.4 1.1 %copy-done.1 = bf16[128,3072]{1,0:T(8,128)(2,1)S(1)} copy-done((bf16[128,3072]{1,0:T(8,128)(2,1)S(1)}, bf16[128,3072]{1,0:T(8,128)(2,1)}, u32[]{:S(2)}) %copy-start.1) | copy-done | bytes 786456
  3.5 53.6 %relay.1 = (bf16[128,3072]{1,0:T(8,128)(2,1)S(1)}, bf16[128,3072]{1,0:T(8,128)(2,1)S(1)}) custom-call(bf16[128,3072]{1,0:T(8,128)(2,1)S(1)} %copy-done, bf16[128,3072]{1,0:T(8,128)(2,1)S(1)} %copy-done.1, bf16[3072,1536]{1,0:T(8,128)(2,1)} %encoder.1, s32[1]{0:T(128)S(6)} %copy.8.lengths), custom_call_target="tpu_custom_call" | custom-call | tf_op jit(solution)/shard_map/relay/pallas_call | solution.py:369
  57.1 0.9 %copy.9 = bf16[128,3072]{1,0:T(8,128)(2,1)} copy(bf16[128,3072]{1,0:T(8,128)(2,1)S(1)} %get-tuple-element.4) | data formatting | bytes 1572864
  58.0 0.9 %copy.10 = bf16[128,3072]{1,0:T(8,128)(2,1)} copy(bf16[128,3072]{1,0:T(8,128)(2,1)S(1)} %get-tuple-element.5) | data formatting | bytes 1572864
Async XLA Ops:
  1.3 1.1 %copy-start = (bf16[128,3072]{1,0:T(8,128)(2,1)S(1)}, bf16[128,3072]{1,0:T(8,128)(2,1)}, u32[]{:S(2)}) copy-start(bf16[128,3072]{1,0:T(8,128)(2,1)} %hidden.1) | copy-start | bytes 2359300
  2.4 1.1 %copy-start.1 = (bf16[128,3072]{1,0:T(8,128)(2,1)S(1)}, bf16[128,3072]{1,0:T(8,128)(2,1)}, u32[]{:S(2)}) copy-start(bf16[128,3072]{1,0:T(8,128)(2,1)} %cotangent.1) | copy-start | bytes 2359300

commit v2 on v1

--- a/solution.py
+++ b/solution.py
@@ -41,6 +41,7 @@
     gradient,
     x,
     enc,
+    turned,
     part,
     part_in,
     colsum,
@@ -57,8 +58,6 @@
     piece_in,
     acc_b,
     acc_r,
-    out_d,
-    out_g,
     load_sem,
     part_ss,
     part_rs,
@@ -76,7 +75,6 @@
     gf_rs,
     piece_ss,
     piece_rs,
-    out_sem,
 ):
     s = lax.axis_index("section")
     t = lax.axis_index("tensor")
@@ -217,6 +215,15 @@
         send_far(1, j).start()
 
     loop(start_second)
+
+    def turn(p, carry):
+        for n in range(SPLIT):
+            turned[p, n] = enc[p, n * CHUNK : (n + 1) * CHUNK, :].T
+        return carry
+
+    acc_b[...] = jnp.zeros(acc_b.shape, F32)
+    acc_r[...] = jnp.zeros(acc_r.shape, F32)
+    lax.fori_loop(0, BLOCKS, turn, 0)
 
     def finish_grad(j):
         send_part(PER + j).wait_recv()
@@ -269,28 +276,21 @@
     for k in range(3):
         send_piece(k).start()
 
-    def decode(acc, buf, p, fresh):
+    def decode(acc, buf, p):
         left = jnp.concatenate([buf[p, 0], buf[p, 1]], axis=1)
 
         def step(n, carry):
-            at = pl.ds(pl.multiple_of(n * CHUNK, CHUNK), CHUNK)
-            d = lax.dot_general(
-                left, enc[p, at, :], (((1,), (1,)), ((), ())), preferred_element_type=F32
-            )
-            acc[n] = acc[n] + d
+            acc[n] = acc[n] + jnp.dot(left, turned[p, n], preferred_element_type=F32)
             return carry
 
         lax.fori_loop(0, SPLIT, step, 0)
-
-    acc_b[...] = jnp.zeros(acc_b.shape, F32)
-    acc_r[...] = jnp.zeros(acc_r.shape, F32)
 
     def middle(j):
         shift(1, j).wait_recv()
         gather_far(1, j).start()
         gather_core(1, j).start()
         gather_core(0, j).wait_recv()
-        decode(acc_b, back, PER + j, False)
+        decode(acc_b, back, PER + j)
         gather_far(0, j).wait_recv()
         pass_core(0, j).start()
 
@@ -298,9 +298,9 @@
 
     def late(j):
         pass_core(0, j).wait_recv()
-        decode(acc_b, back, j, False)
+        decode(acc_b, back, j)
         gather_core(1, j).wait_recv()
-        decode(acc_r, recv, PER + j, False)
+        decode(acc_r, recv, PER + j)
         gather_far(1, j).wait_recv()
         pass_core(1, j).start()
 
@@ -311,14 +311,6 @@
     pieces = piece_out[...] + piece_in[0] + piece_in[1] + piece_in[2]
     first = column(pieces[0:1] / MODEL_WIDTH)
     second = column(pieces[1:2] / MODEL_WIDTH)
-
-    def to_gradient(n):
-        at = pl.ds(pl.multiple_of(n * CHUNK, CHUNK), CHUNK)
-        return pltpu.make_async_copy(out_g.at[n], gradient.at[:, at], out_sem.at[n])
-
-    def to_decoded(n):
-        at = pl.ds(pl.multiple_of(n * CHUNK, CHUNK), CHUNK)
-        return pltpu.make_async_copy(out_d.at[n], decoded.at[:, at], out_sem.at[SPLIT + n])
 
     for n in range(SPLIT):
         for i in range(CHUNK // HALF):
@@ -326,19 +318,15 @@
             v = x[ROWS : 2 * ROWS, lo : lo + HALF].astype(F32)
             normed = (v - mean) * rstd
             g = acc_b[n, :, i * HALF : (i + 1) * HALF] * mask
-            out_g[n, :, i * HALF : (i + 1) * HALF] = (
-                rstd * (g - first - normed * second)
-            ).astype(BF16)
-        to_gradient(n).start()
+            gradient[:, lo : lo + HALF] = (rstd * (g - first - normed * second)).astype(BF16)
 
     def final(j):
         pass_core(1, j).wait_recv()
-        decode(acc_r, recv, j, False)
+        decode(acc_r, recv, j)
 
     loop(final)
     for n in range(SPLIT):
-        out_d[n] = acc_r[n].astype(BF16)
-        to_decoded(n).start()
+        decoded[:, n * CHUNK : (n + 1) * CHUNK] = acc_r[n].astype(BF16)
 
     def drain(p, carry):
         send_part(p).wait_send()
@@ -358,13 +346,11 @@
     for k in range(3):
         send_stat(k).wait_send()
         send_piece(k).wait_send()
-    for n in range(SPLIT):
-        to_gradient(n).wait()
-        to_decoded(n).wait()
 
 
 def shards(sections, hidden, cotangent, encoder, lengths):
-    any_space = pl.BlockSpec(memory_space=pl.ANY)
+    hbm = pl.BlockSpec(memory_space=pltpu.HBM)
+    vmem = pl.BlockSpec(memory_space=pltpu.VMEM)
     sems = lambda n: pltpu.SemaphoreType.DMA((n,))
     return pl.pallas_call(
         functools.partial(kernel, sections),
@@ -372,11 +358,12 @@
             jax.ShapeDtypeStruct((ROWS, DEPTH), BF16),
             jax.ShapeDtypeStruct((ROWS, DEPTH), BF16),
         ),
-        in_specs=[any_space, any_space, any_space, pl.BlockSpec(memory_space=pltpu.SMEM)],
-        out_specs=(any_space, any_space),
+        in_specs=[hbm, hbm, hbm, pl.BlockSpec(memory_space=pltpu.SMEM)],
+        out_specs=(vmem, vmem),
         scratch_shapes=[
             pltpu.VMEM((2 * ROWS + 16, DEPTH), BF16),
             pltpu.VMEM((BLOCKS, DEPTH, BLOCK), BF16),
+            pltpu.VMEM((BLOCKS, SPLIT, BLOCK, CHUNK), BF16),
             pltpu.VMEM((BLOCKS, 2, 2 * ROWS, HALF), F32),
             pltpu.VMEM((BLOCKS, 2 * ROWS, HALF), F32),
             pltpu.VMEM((BLOCKS, 2, 8, HALF), F32),
@@ -393,8 +380,6 @@
             pltpu.VMEM((3, 8, HALF), F32),
             pltpu.VMEM((SPLIT, ROWS, CHUNK), F32),
             pltpu.VMEM((SPLIT, ROWS, CHUNK), F32),
-            pltpu.VMEM((SPLIT, ROWS, CHUNK), BF16),
-            pltpu.VMEM((SPLIT, ROWS, CHUNK), BF16),
             sems(2 + BLOCKS),
             sems(BLOCKS),
             sems(BLOCKS),
@@ -412,13 +397,12 @@
             sems(2 * PER),
             sems(3),
             sems(3),
-            sems(2 * SPLIT),
         ],
         compiler_params=pltpu.CompilerParams(
             collective_id=0, has_side_effects=True, vmem_limit_bytes=48 * 1024 * 1024
         ),
         name="relay",
-    )(hidden, cotangent, encoder, lengths)
+    )(*[pltpu.with_memory_space_constraint(v, pltpu.HBM) for v in (hidden, cotangent, encoder)], lengths)
 
 
 def solution(mesh):

time: 59.1 us -> 54.5 us (0.922)
  Pallas kernels: 53.6 us -> 51.3 us
  local copies, waits for them, and re-layouts: 4.02 us -> 1.76 us
    pallas_call x1, Pallas kernels: 53.6 us -> 51.3 us  [shards(): pl.pallas_call(functools.partial(kernel, sections), out_shape=(jax.ShapeD...]
    unnamed x6 -> x2, local copies, waits for them, and re-layouts: 4.02 us -> 1.76 us
where the time goes in v2:
time: 54.5 us; the launch traced here: 54.3 us
  Pallas kernels  51.3 us (94%)
  local copies, waits for them, and re-layouts  1.76 us (3%)
  between operations  1.29 us (2%)
    pallas_call x1, Pallas kernels, shards(): pl.pallas_call(functools.partial(kernel, sections), out_shape=(jax.ShapeD...  51.3 us
    unnamed x2, local copies, waits for them, and re-layouts  1.76 us

profile of v2, /device:TPU:1, one launch (start us, length us, event | category | flops | bytes accessed | tf_op | source)
XLA Modules:
  0.0 54.3 jit_solution(17937639978559520626)
XLA Ops:
  1.3 51.3 %relay.1 = (bf16[128,3072]{1,0:T(8,128)(2,1)S(1)}, bf16[128,3072]{1,0:T(8,128)(2,1)S(1)}) custom-call(bf16[128,3072]{1,0:T(8,128)(2,1)} %hidden.1, bf16[128,3072]{1,0:T(8,128)(2,1)} %cotangent.1, bf16[3072,1536]{1,0:T(8,128)(2,1)} %encoder.1, s32[1]{0:T(128)S(6)} %copy.8.lengths), custom_call_target="tpu_custom_call" | custom-call | tf_op jit(solution)/shard_map/relay/pallas_call | solution.py:355
  52.6 0.9 %copy.9 = bf16[128,3072]{1,0:T(8,128)(2,1)} copy(bf16[128,3072]{1,0:T(8,128)(2,1)S(1)} %get-tuple-element.4) | data formatting | bytes 1572864
  53.4 0.9 %copy.10 = bf16[128,3072]{1,0:T(8,128)(2,1)} copy(bf16[128,3072]{1,0:T(8,128)(2,1)S(1)} %get-tuple-element.5) | data formatting | bytes 1572864

commit v3 on v2

--- a/solution.py
+++ b/solution.py
@@ -250,7 +250,15 @@
 
     first = jnp.zeros((ROWS, HALF), F32)
     second = jnp.zeros((ROWS, HALF), F32)
-    for j in range(PER):
+    last = lax.rem(s, 12) == 11
+
+    def start_back(j):
+        shift(0, j).wait_recv()
+        gather_far(0, j).start()
+        gather_core(0, j).start()
+
+    for j in range(PER):
+        pl.when(jnp.logical_not(last))(functools.partial(start_back, j))
         send_far(1, j).wait_recv()
         full = (
             part[PER + j, c, ROWS : 2 * ROWS, :]
@@ -263,9 +271,8 @@
         zs[j] = z
         ls[j] = (mask * z).astype(BF16)
         shift(1, j).start()
-        shift(0, j).wait_recv()
-        gather_far(0, j).start()
-        gather_core(0, j).start()
+    for j in range(PER):
+        pl.when(last)(functools.partial(start_back, j))
     for j in range(PER):
         b = back[PER + j, c].astype(F32)
         first = first + b * tile[j : j + 1]
@@ -285,24 +292,23 @@
 
         lax.fori_loop(0, SPLIT, step, 0)
 
-    def middle(j):
+    for j in range(PER):
         shift(1, j).wait_recv()
         gather_far(1, j).start()
         gather_core(1, j).start()
+        if j > 0:
+            gather_far(0, j - 1).wait_recv()
+            pass_core(0, j - 1).start()
         gather_core(0, j).wait_recv()
         decode(acc_b, back, PER + j)
-        gather_far(0, j).wait_recv()
-        pass_core(0, j).start()
-
-    loop(middle)
+    gather_far(0, PER - 1).wait_recv()
+    pass_core(0, PER - 1).start()
 
     def late(j):
         pass_core(0, j).wait_recv()
         decode(acc_b, back, j)
         gather_core(1, j).wait_recv()
         decode(acc_r, recv, PER + j)
-        gather_far(1, j).wait_recv()
-        pass_core(1, j).start()
 
     loop(late)
 
@@ -320,13 +326,17 @@
             g = acc_b[n, :, i * HALF : (i + 1) * HALF] * mask
             gradient[:, lo : lo + HALF] = (rstd * (g - first - normed * second)).astype(BF16)
 
-    def final(j):
-        pass_core(1, j).wait_recv()
-        decode(acc_r, recv, j)
-
-    loop(final)
+    for j in range(PER):
+        gather_far(1, j).wait_recv()
+        pass_core(1, j).start()
+        if j > 0:
+            pass_core(1, j - 1).wait_recv()
+            decode(acc_r, recv, j - 1)
+    pass_core(1, PER - 1).wait_recv()
+    left = jnp.concatenate([recv[PER - 1, 0], recv[PER - 1, 1]], axis=1)
     for n in range(SPLIT):
-        decoded[:, n * CHUNK : (n + 1) * CHUNK] = acc_r[n].astype(BF16)
+        d = jnp.dot(left, turned[PER - 1, n], preferred_element_type=F32)
+        decoded[:, n * CHUNK : (n + 1) * CHUNK] = (acc_r[n] + d).astype(BF16)
 
     def drain(p, carry):
         send_part(p).wait_send()

time: 54.5 us -> 53.7 us (0.985)
  Pallas kernels: 51.3 us -> 50.5 us
    pallas_call x1, Pallas kernels: 51.3 us -> 50.5 us  [shards(): pl.pallas_call(functools.partial(kernel, sections), out_shape=(jax.ShapeD...]
where the time goes in v3:
time: 53.7 us; the launch traced here: 53.6 us
  Pallas kernels  50.5 us (94%)
  local copies, waits for them, and re-layouts  1.76 us (3%)
  between operations  1.29 us (2%)
    pallas_call x1, Pallas kernels, shards(): pl.pallas_call(functools.partial(kernel, sections), out_shape=(jax.ShapeD...  50.5 us
    unnamed x2, local copies, waits for them, and re-layouts  1.76 us

profile of v3, /device:TPU:1, one launch (start us, length us, event | category | flops | bytes accessed | tf_op | source)
XLA Modules:
  0.0 53.6 jit_solution(15991324059597553864)
XLA Ops:
  1.3 50.5 %relay.1 = (bf16[128,3072]{1,0:T(8,128)(2,1)S(1)}, bf16[128,3072]{1,0:T(8,128)(2,1)S(1)}) custom-call(bf16[128,3072]{1,0:T(8,128)(2,1)} %hidden.1, bf16[128,3072]{1,0:T(8,128)(2,1)} %cotangent.1, bf16[3072,1536]{1,0:T(8,128)(2,1)} %encoder.1, s32[1]{0:T(128)S(6)} %copy.8.lengths), custom_call_target="tpu_custom_call" | custom-call | tf_op jit(solution)/shard_map/relay/pallas_call | solution.py:365
  51.8 0.9 %copy.9 = bf16[128,3072]{1,0:T(8,128)(2,1)} copy(bf16[128,3072]{1,0:T(8,128)(2,1)S(1)} %get-tuple-element.4) | data formatting | bytes 1572864
  52.7 0.9 %copy.10 = bf16[128,3072]{1,0:T(8,128)(2,1)} copy(bf16[128,3072]{1,0:T(8,128)(2,1)S(1)} %get-tuple-element.5) | data formatting | bytes 1572864

commit v4 on v3

--- a/solution.py
+++ b/solution.py
@@ -37,8 +37,10 @@
     cotangent,
     encoder,
     lengths,
-    decoded,
     gradient,
+    acc_r,
+    left,
+    turned_last,
     x,
     enc,
     turned,
@@ -57,7 +59,6 @@
     piece_out,
     piece_in,
     acc_b,
-    acc_r,
     load_sem,
     part_ss,
     part_rs,
@@ -224,6 +225,8 @@
     acc_b[...] = jnp.zeros(acc_b.shape, F32)
     acc_r[...] = jnp.zeros(acc_r.shape, F32)
     lax.fori_loop(0, BLOCKS, turn, 0)
+    for n in range(SPLIT):
+        turned_last[n] = turned[PER - 1, n]
 
     def finish_grad(j):
         send_part(PER + j).wait_recv()
@@ -284,10 +287,10 @@
         send_piece(k).start()
 
     def decode(acc, buf, p):
-        left = jnp.concatenate([buf[p, 0], buf[p, 1]], axis=1)
+        block = jnp.concatenate([buf[p, 0], buf[p, 1]], axis=1)
 
         def step(n, carry):
-            acc[n] = acc[n] + jnp.dot(left, turned[p, n], preferred_element_type=F32)
+            acc[n] = acc[n] + jnp.dot(block, turned[p, n], preferred_element_type=F32)
             return carry
 
         lax.fori_loop(0, SPLIT, step, 0)
@@ -333,10 +336,8 @@
             pass_core(1, j - 1).wait_recv()
             decode(acc_r, recv, j - 1)
     pass_core(1, PER - 1).wait_recv()
-    left = jnp.concatenate([recv[PER - 1, 0], recv[PER - 1, 1]], axis=1)
-    for n in range(SPLIT):
-        d = jnp.dot(left, turned[PER - 1, n], preferred_element_type=F32)
-        decoded[:, n * CHUNK : (n + 1) * CHUNK] = (acc_r[n] + d).astype(BF16)
+    left[:, 0:HALF] = recv[PER - 1, 0]
+    left[:, HALF:BLOCK] = recv[PER - 1, 1]
 
     def drain(p, carry):
         send_part(p).wait_send()
@@ -358,18 +359,35 @@
         send_piece(k).wait_send()
 
 
+def finish_kernel(gradient, acc, left, turned_last, decoded_out, gradient_out, staged, sem):
+    whole = pltpu.make_async_copy(gradient, gradient_out, sem.at[SPLIT])
+    whole.start()
+    copies = []
+    for n in range(SPLIT):
+        d = jnp.dot(left[...], turned_last[n], preferred_element_type=F32)
+        staged[n] = (acc[n] + d).astype(BF16)
+        at = pl.ds(n * CHUNK, CHUNK)
+        copies.append(pltpu.make_async_copy(staged.at[n], decoded_out.at[:, at], sem.at[n]))
+        copies[-1].start()
+    for copy in copies:
+        copy.wait()
+    whole.wait()
+
+
 def shards(sections, hidden, cotangent, encoder, lengths):
     hbm = pl.BlockSpec(memory_space=pltpu.HBM)
     vmem = pl.BlockSpec(memory_space=pltpu.VMEM)
     sems = lambda n: pltpu.SemaphoreType.DMA((n,))
-    return pl.pallas_call(
+    gradient, acc, left, turned_last = pl.pallas_call(
         functools.partial(kernel, sections),
         out_shape=(
             jax.ShapeDtypeStruct((ROWS, DEPTH), BF16),
-            jax.ShapeDtypeStruct((ROWS, DEPTH), BF16),
+            jax.ShapeDtypeStruct((SPLIT, ROWS, CHUNK), F32),
+            jax.ShapeDtypeStruct((ROWS, BLOCK), BF16),
+            jax.ShapeDtypeStruct((SPLIT, BLOCK, CHUNK), BF16),
         ),
         in_specs=[hbm, hbm, hbm, pl.BlockSpec(memory_space=pltpu.SMEM)],
-        out_specs=(vmem, vmem),
+        out_specs=(vmem,) * 4,
         scratch_shapes=[
             pltpu.VMEM((2 * ROWS + 16, DEPTH), BF16),
             pltpu.VMEM((BLOCKS, DEPTH, BLOCK), BF16),
@@ -389,7 +407,6 @@
             pltpu.VMEM((8, HALF), F32),
             pltpu.VMEM((3, 8, HALF), F32),
             pltpu.VMEM((SPLIT, ROWS, CHUNK), F32),
-            pltpu.VMEM((SPLIT, ROWS, CHUNK), F32),
             sems(2 + BLOCKS),
             sems(BLOCKS),
             sems(BLOCKS),
@@ -413,6 +430,21 @@
         ),
         name="relay",
     )(*[pltpu.with_memory_space_constraint(v, pltpu.HBM) for v in (hidden, cotangent, encoder)], lengths)
+    return pl.pallas_call(
+        finish_kernel,
+        out_shape=(
+            jax.ShapeDtypeStruct((ROWS, DEPTH), BF16),
+            jax.ShapeDtypeStruct((ROWS, DEPTH), BF16),
+        ),
+        in_specs=[vmem] * 4,
+        out_specs=(hbm, hbm),
+        scratch_shapes=[
+            pltpu.VMEM((SPLIT, ROWS, CHUNK), BF16),
+            sems(SPLIT + 1),
+        ],
+        compiler_params=pltpu.CompilerParams(vmem_limit_bytes=16 * 1024 * 1024),
+        name="finish",
+    )(gradient, acc, left, turned_last)
 
 
 def solution(mesh):

time: 53.7 us -> 52.8 us (0.983)
  local copies, waits for them, and re-layouts: 1.76 us -> 0 us
  Pallas kernels: 50.5 us -> 51.3 us
    unnamed x2 -> x0, local copies, waits for them, and re-layouts: 1.76 us -> none
    pallas_call x0 -> x1, Pallas kernels: none -> 1.19 us  [shards(): pl.pallas_call(finish_kernel, out_shape=(jax.ShapeDtypeStruct((ROWS, DEPT...]
where the time goes in v4:
time: 52.8 us; the launch traced here: 52.6 us
  Pallas kernels  51.3 us (97%)
  between operations  1.28 us (2%)
    pallas_call x1, Pallas kernels, shards(): pl.pallas_call(functools.partial(kernel, sections), out_shape=(jax.ShapeD...  50.1 us
    pallas_call x1, Pallas kernels, shards(): pl.pallas_call(finish_kernel, out_shape=(jax.ShapeDtypeStruct((ROWS, DEPT...  1.19 us

profile of v4, /device:TPU:1, one launch (start us, length us, event | category | flops | bytes accessed | tf_op | source)
XLA Modules:
  0.0 52.6 jit_solution(8505896793002850619)
XLA Ops:
  1.3 50.1 %relay.1 = (bf16[128,3072]{1,0:T(8,128)(2,1)S(1)}, f32[4,128,768]{2,1,0:T(8,128)S(1)}, bf16[128,256]{1,0:T(8,128)(2,1)S(1)}, bf16[4,256,768]{2,1,0:T(8,128)(2,1)S(1)}) custom-call(bf16[128,3072]{1,0:T(8,128)(2,1)} %hidden.1, bf16[128,3072]{1,0:T(8,128)(2,1)} %cotangent.1, bf16[3072,1536]{1,0:T(8,128)(2,1)} %encoder.1, s32[1]{0:T(128)S(6)} %copy.6.lengths), custom_call_target="tpu_custom_call" | custom-call | tf_op jit(solution)/shard_map/relay/pallas_call | solution.py:381
  51.4 1.2 %finish.1 = (bf16[128,3072]{1,0:T(8,128)(2,1)}, bf16[128,3072]{1,0:T(8,128)(2,1)}) custom-call(bf16[128,3072]{1,0:T(8,128)(2,1)S(1)} %get-tuple-element.6.gradient, f32[4,128,768]{2,1,0:T(8,128)S(1)} %get-tuple-element.7.acc, bf16[128,256]{1,0:T(8,128)(2,1)S(1)} %get-tuple-element.8.left, bf16[4,256,768]{2,1,0:T(8,128)(2,1)S(1)} %get-tuple-element.9.turned_last), custom_call_target="tpu_custom_call" | custom-call | tf_op jit(solution)/shard_map/finish/pallas_call | solution.py:433
